TPU v7x, 32 devices: a whole 2x2x4 slice. The times are simulated.
32 devices in a mesh: curve: 8 (over z, x), head: 4 (over y, core).
Axes of the slice: x: 2, y: 2, z: 4, core: 2. Of those that a mesh axis runs over, the one named last changes fastest.
Arguments:
- points: bfloat16 [16384, 1024], P(('curve', 'head')), may hold values from -6 to 6
- order: int32 [32, 512], P(('curve', 'head')), may hold values from 0 to 511, each once within a row
- scan_ids: int32 [16384], P(('curve', 'head')), may hold values from 0 to 3
- ln_gain: float32 [2, 1024], replicated, may hold values from 0.25 to 1.75
- w_qkv: bfloat16 [2, 1024, 3072], P(None, None, 'head'), may hold values from -7 to 7, as said below
- w_out: bfloat16 [2, 1024, 1024], P(None, 'head'), may hold values from -0.1875 to 0.1875
Outputs:
- refined: bfloat16 [16384, 1024], P(('curve', 'head'))
Inputs may be any that keep to these rules, and one draw needn't show every extreme that they name: `order`: row b is a permutation of the 512 rows of block b. `w_qkv`: columns ordered by head, then query, key, value, then entry.
All inputs are finite; a program needn't handle non-finite values.
Results may differ from a plain program's by a relative error of at most 0.01.
Values may be sent and summed in bfloat16 or wider, within the bound.
A program may use at most 64 MiB of HBM per device.

v0:
```python
import jax
import jax.numpy as jnp
from jax import lax
from jax.sharding import PartitionSpec as P

HEAD_DIM = 64
PATCH = 1024
EPSILON = 1e-05


def extended(array, sides, width):
    for axis, dim in sides:
        peers, length = (lax.axis_size(axis), array.shape[dim])
        up = [(i, (i + 1) % peers) for i in range(peers)]
        down = [(j, i) for i, j in up]
        last = lax.slice_in_dim(array, length - width, length, axis=dim)
        first = lax.slice_in_dim(array, 0, width, axis=dim)
        before = lax.ppermute(last, axis, up)
        after = lax.ppermute(first, axis, down)
        array = jnp.concatenate([before, array, after], axis=dim)
    return array


def layer_norm(rows, gain):
    values = rows.astype(jnp.float32)
    center = values - jnp.mean(values, axis=-1, keepdims=True)
    spread = jnp.mean(center * center, axis=-1, keepdims=True)
    return (center * lax.rsqrt(spread + EPSILON) * gain).astype(jnp.bfloat16)


def plain_window(first_row):
    return first_row // PATCH * PATCH


def centred_window(first_row):
    return (first_row + PATCH // 2) // PATCH * PATCH


def attend(queries, keys, values, query_tags, key_tags, window_of):
    block_rows = PATCH // 2
    blocks_count = queries.shape[0] // block_rows

    def one_block(block_index):
        first_row = block_index * block_rows
        query_block = lax.dynamic_slice_in_dim(queries, first_row, block_rows, 0)
        tags_block = lax.dynamic_slice_in_dim(query_tags, first_row, block_rows, 0)
        first_key = window_of(first_row)
        key_block = lax.dynamic_slice_in_dim(keys, first_key, PATCH, 0)
        value_block = lax.dynamic_slice_in_dim(values, first_key, PATCH, 0)
        key_block_tags = lax.dynamic_slice_in_dim(key_tags, first_key, PATCH, 0)
        scores = jnp.einsum(
            "qhd,khd->hqk", query_block, key_block, preferred_element_type=jnp.float32
        ) * HEAD_DIM ** (-0.5)
        allowed = tags_block[:, None] == key_block_tags[None, :]
        scores = jnp.where(allowed[None], scores, -jnp.inf)
        row_max = jnp.max(scores, axis=-1, keepdims=True)
        expo = jnp.exp(scores - row_max)
        probs = (expo / jnp.sum(expo, axis=-1, keepdims=True)).astype(jnp.bfloat16)
        result = jnp.einsum("hqk,khd->qhd", probs, value_block, preferred_element_type=jnp.float32)
        return result.astype(jnp.bfloat16)

    outputs = lax.map(one_block, jnp.arange(blocks_count))
    return outputs.reshape(queries.shape[0], -1)


def on_device(points, order, scan_ids, ln_gain, w_qkv, w_out):
    stream = points[order[0]]
    range_ids = lax.all_gather(scan_ids, "head", axis=0, tiled=True)
    span_rows = range_ids.shape[0]
    heads_local = w_qkv.shape[2] // (3 * HEAD_DIM)
    half_patch = PATCH // 2
    for layer_index in range(2):
        normed = layer_norm(stream, ln_gain[layer_index])
        weights_here = w_qkv[layer_index]
        qkv_span = jnp.dot(
            lax.all_gather(normed, "head", axis=0, tiled=True),
            weights_here,
            preferred_element_type=jnp.float32,
        ).astype(jnp.bfloat16)
        pieces = qkv_span.reshape(span_rows, heads_local, 3, HEAD_DIM)
        if layer_index == 0:
            attended = attend(
                pieces[:, :, 0],
                pieces[:, :, 1],
                pieces[:, :, 2],
                range_ids,
                range_ids,
                plain_window,
            )
        else:
            tags_float = range_ids.astype(jnp.bfloat16)
            kv_flat = pieces[:, :, 1:].reshape(span_rows, heads_local * 2 * HEAD_DIM)
            wide_kv, wide_tags = (
                extended(kv_flat, (("curve", 0),), half_patch),
                extended(tags_float, (("curve", 0),), half_patch),
            )
            wide_pieces = wide_kv.reshape(-1, heads_local, 2, HEAD_DIM)
            attended = attend(
                pieces[:, :, 0],
                wide_pieces[:, :, 0],
                wide_pieces[:, :, 1],
                range_ids,
                wide_tags.astype(jnp.int32),
                centred_window,
            )
        heads_rows = lax.all_to_all(attended, "head", split_axis=0, concat_axis=1, tiled=True)
        update = jnp.dot(
            heads_rows,
            lax.all_gather(w_out[layer_index], "head", axis=0, tiled=True),
            preferred_element_type=jnp.float32,
        )
        stream = (stream.astype(jnp.float32) + update).astype(jnp.bfloat16)
    return stream


def solution(mesh):
    in_specs = (
        P(("curve", "head"), None),
        P(("curve", "head"), None),
        P(("curve", "head")),
        P(),
        P(None, None, "head"),
        P(None, "head", None),
    )
    out_specs = P(("curve", "head"), None)
    return jax.shard_map(
        on_device, mesh=mesh, in_specs=in_specs, out_specs=out_specs, check_vma=False
    )
```

profile of v0, /device:TPU:0, one launch (start us, length us, event | category | flops | bytes accessed | tf_op | source)
XLA Modules:
  0.0 295.6 jit_solution(13849537120225569016)
XLA Ops:
  6.5 0.8 compare_select_fusion
  7.3 0.5 copy-done
  7.8 2.0 gather_fusion
  10.1 0.4 fusion.67
  10.5 1.3 fusion.69
  12.0 1.1 fusion.103
  13.1 6.2 %all-gather.2 = s32[4,1,512]{2,1,0:T(1,128)S(1)} all-gather(s32[1,1,512]{2,1,0:T(1,128)S(1)} %bitcast.103), channel_id=1, replica_groups=mesh['curve'=8,'head'=4] {'head'}, dimensions={0}, use_global_device_ids=true | all-gather | bytes 10240 | tf_op jit(solution)/shard_map/all_gather | solution.py:68
  19.3 29.9 %all-gather.8.cloned.1.call-done = bf16[2048,1024]{1,0:T(8,128)(2,1)} async-done(((bf16[512,1024]{1,0:T(8,128)(2,1)}), bf16[2048,1024]{1,0:T(8,128)(2,1)}) %all-gather.8.cloned.1.call-update) | async-done | bytes 4194320 | tf_op jit(solution)/shard_map/all_gather | solution.py:76
  49.2 6.1 %convolution_convert_fusion.1 = bf16[2048,768]{0,1:T(8,128)(2,1)S(1)} fusion(bf16[2048,1024]{1,0:T(8,128)(2,1)} %all-gather.8.cloned.1.call-done, bf16[2,1024,768]{2,1,0:T(8,128)(2,1)} %param.14), kind=kOutput, calls=%fused_computation.52 | convolution fusion | flops 3222798336 | bytes 8912896 | tf_op jit(solution)/shard_map/dot_general | solution.py:75
  55.4 1.7 slice_bitcast_fusion.3
  57.0 1.1 broadcast.125.clone
  58.1 58.1 %while.24 = (s32[]{:T(128)}, bf16[4,512,4,64]{1,3,2,0:T(8,128)(2,1)}, s32[4]{0:T(128)S(1)}, bf16[2048,4,64]{0,2,1:T(8,128)(2,1)}, s32[2048]{0:T(1024)S(1)}, /*in...) while((s32[]{:T(128)}, ...), condition=%wide.region_5.6_spmd, body=%wide.region_2.5_spmd.sunk | while | flops 550110208 | bytes 19434388 | solution.py:62
  58.1 0.6 dynamic_slice.136
  59.5 0.4 broadcast_compare_fusion.4
  59.9 7.0 %fusion.123 = (f32[4,512]{1,0:T(4,128)S(1)}, f32[4,512,1024]{2,1,0:T(8,128)}) fusion(pred[512,1024]{1,0:T(8,128)(4,1)S(1)} %broadcast_compare_fusion.4, bf16[2048,4,64]{0,2,1:T(8,128)(2,1)S(1)} %get-tuple-element.384, s32[]{:T(128)S(6)} %select_n.99, bf16[2048,4,64]{0,2,1:T(8,128)(2,1)} %get-tuple-element.383, s32[]{:T(128)S(6)} %select_n.100), kind=kOutput, calls=%fused_computation.93.clone.1 | convolution fusion | flops 276825088 | bytes 9707528 | tf_op jit(solution)/shard_map/while/body/eval_jaxpr/sub | solution.py:57
  66.9 5.8 %fusion.124 = bf16[4,512,4,64]{1,3,2,0:T(8,128)(2,1)} fusion(bf16[4,512,4,64]{1,3,2,0:T(8,128)(2,1)} %get-tuple-element.364, s32[]{:T(128)} %get-tuple-element.363, f32[4,512,1024]{2,1,0:T(8,128)} %get-tuple-element.336, f32[4,512]{1,0:T(4,128)S(1)} %get-tuple-element.337, bf16[2048,4,64]{0,2,1:T(8,128)(2,1)} %get-tuple-element.381, s32[]{:T(128)S(6)} %select_n.99), kind=kOutput, calls=%fused_computation.12.clone.1 | convolution fusion | flops 272760832 | bytes 9183748 | tf_op jit(solution)/shard_map/while/body/eval_jaxpr/hqk,khd->qhd/dot_general | solution.py:59
  72.7 0.6 dynamic_slice.136
  74.0 0.4 broadcast_compare_fusion.4
  74.4 7.0 %fusion.123 = (f32[4,512]{1,0:T(4,128)S(1)}, f32[4,512,1024]{2,1,0:T(8,128)}) fusion(pred[512,1024]{1,0:T(8,128)(4,1)S(1)} %broadcast_compare_fusion.4, bf16[2048,4,64]{0,2,1:T(8,128)(2,1)S(1)} %get-tuple-element.384, s32[]{:T(128)S(6)} %select_n.99, bf16[2048,4,64]{0,2,1:T(8,128)(2,1)} %get-tuple-element.383, s32[]{:T(128)S(6)} %select_n.100), kind=kOutput, calls=%fused_computation.93.clone.1 | convolution fusion | flops 276825088 | bytes 9707528 | tf_op jit(solution)/shard_map/while/body/eval_jaxpr/sub | solution.py:57
  81.4 5.7 %fusion.124 = bf16[4,512,4,64]{1,3,2,0:T(8,128)(2,1)} fusion(bf16[4,512,4,64]{1,3,2,0:T(8,128)(2,1)} %get-tuple-element.364, s32[]{:T(128)} %get-tuple-element.363, f32[4,512,1024]{2,1,0:T(8,128)} %get-tuple-element.336, f32[4,512]{1,0:T(4,128)S(1)} %get-tuple-element.337, bf16[2048,4,64]{0,2,1:T(8,128)(2,1)} %get-tuple-element.381, s32[]{:T(128)S(6)} %select_n.99), kind=kOutput, calls=%fused_computation.12.clone.1 | convolution fusion | flops 272760832 | bytes 9183748 | tf_op jit(solution)/shard_map/while/body/eval_jaxpr/hqk,khd->qhd/dot_general | solution.py:59
  87.2 0.6 dynamic_slice.136
  88.6 0.4 broadcast_compare_fusion.4
  88.9 7.0 %fusion.123 = (f32[4,512]{1,0:T(4,128)S(1)}, f32[4,512,1024]{2,1,0:T(8,128)}) fusion(pred[512,1024]{1,0:T(8,128)(4,1)S(1)} %broadcast_compare_fusion.4, bf16[2048,4,64]{0,2,1:T(8,128)(2,1)S(1)} %get-tuple-element.384, s32[]{:T(128)S(6)} %select_n.99, bf16[2048,4,64]{0,2,1:T(8,128)(2,1)} %get-tuple-element.383, s32[]{:T(128)S(6)} %select_n.100), kind=kOutput, calls=%fused_computation.93.clone.1 | convolution fusion | flops 276825088 | bytes 9707528 | tf_op jit(solution)/shard_map/while/body/eval_jaxpr/sub | solution.py:57
  95.9 5.7 %fusion.124 = bf16[4,512,4,64]{1,3,2,0:T(8,128)(2,1)} fusion(bf16[4,512,4,64]{1,3,2,0:T(8,128)(2,1)} %get-tuple-element.364, s32[]{:T(128)} %get-tuple-element.363, f32[4,512,1024]{2,1,0:T(8,128)} %get-tuple-element.336, f32[4,512]{1,0:T(4,128)S(1)} %get-tuple-element.337, bf16[2048,4,64]{0,2,1:T(8,128)(2,1)} %get-tuple-element.381, s32[]{:T(128)S(6)} %select_n.99), kind=kOutput, calls=%fused_computation.12.clone.1 | convolution fusion | flops 272760832 | bytes 9183748 | tf_op jit(solution)/shard_map/while/body/eval_jaxpr/hqk,khd->qhd/dot_general | solution.py:59
  101.7 0.6 dynamic_slice.136
  103.1 0.4 broadcast_compare_fusion.4
  103.4 7.0 %fusion.123 = (f32[4,512]{1,0:T(4,128)S(1)}, f32[4,512,1024]{2,1,0:T(8,128)}) fusion(pred[512,1024]{1,0:T(8,128)(4,1)S(1)} %broadcast_compare_fusion.4, bf16[2048,4,64]{0,2,1:T(8,128)(2,1)S(1)} %get-tuple-element.384, s32[]{:T(128)S(6)} %select_n.99, bf16[2048,4,64]{0,2,1:T(8,128)(2,1)} %get-tuple-element.383, s32[]{:T(128)S(6)} %select_n.100), kind=kOutput, calls=%fused_computation.93.clone.1 | convolution fusion | flops 276825088 | bytes 9707528 | tf_op jit(solution)/shard_map/while/body/eval_jaxpr/sub | solution.py:57
  110.5 5.7 %fusion.124 = bf16[4,512,4,64]{1,3,2,0:T(8,128)(2,1)} fusion(bf16[4,512,4,64]{1,3,2,0:T(8,128)(2,1)} %get-tuple-element.364, s32[]{:T(128)} %get-tuple-element.363, f32[4,512,1024]{2,1,0:T(8,128)} %get-tuple-element.336, f32[4,512]{1,0:T(4,128)S(1)} %get-tuple-element.337, bf16[2048,4,64]{0,2,1:T(8,128)(2,1)} %get-tuple-element.381, s32[]{:T(128)S(6)} %select_n.99), kind=kOutput, calls=%fused_computation.12.clone.1 | convolution fusion | flops 272760832 | bytes 9183748 | tf_op jit(solution)/shard_map/while/body/eval_jaxpr/hqk,khd->qhd/dot_general | solution.py:59
  116.2 3.5 %all-to-all-start = ((bf16[4,512,256]{1,2,0:T(8,128)(2,1)}), bf16[4,512,256]{1,2,0:T(8,128)(2,1)S(1)}, u32[]{:S(2)}, u32[]{:S(2)}) async-start(bf16[4,512,256]{1,2,0:T(8,128)(2,1)} %bitcast.16), calls=%async_computation | async-start | bytes 2097152 | tf_op jit(solution)/shard_map/all_to_all | solution.py:106
  120.0 14.1 %all-to-all-done = bf16[4,512,256]{1,2,0:T(8,128)(2,1)S(1)} async-done(((bf16[4,512,256]{1,2,0:T(8,128)(2,1)}), bf16[4,512,256]{1,2,0:T(8,128)(2,1)S(1)}, u32[]{:S(2)}, u32[]{:S(2)}) %all-to-all-start) | async-done | bytes 1048608 | tf_op jit(solution)/shard_map/all_to_all | solution.py:106
  134.1 2.9 convert_reduce_fusion
  137.1 0.4 fusion.64
  137.5 1.4 fusion.66
  139.0 1.5 collective-permute-start.2
  140.5 3.3 %collective-permute-start.3 = (bf16[512]{0:T(512)(128)(2,1)S(1)}, bf16[512]{0:T(512)(128)(2,1)S(1)}, u32[]{:S(2)}, u32[]{:S(2)}) collective-permute-start(bf16[512]{0:T(512)(128)(2,1)S(1)} %get-tuple-element.245), channel_id=1, source_target_pairs={{4,0},{8,4},{12,8},{16,12},{20,16},{24,20},{28,24},{0,28},{5,1},{9... | collective-permute-start | bytes 3080 | tf_op jit(solution)/shard_map/ppermute | solution.py:19
  143.8 29.7 %all-gather.10.cloned.1.call-done = bf16[2048,1024]{1,0:T(8,128)(2,1)} async-done(((bf16[512,1024]{1,0:T(8,128)(2,1)}), bf16[2048,1024]{1,0:T(8,128)(2,1)}) %all-gather.10.cloned.1.call-update) | async-done | bytes 4194320 | tf_op jit(solution)/shard_map/all_gather | solution.py:76
  173.5 6.1 %convolution_convert_fusion = bf16[2048,768]{0,1:T(8,128)(2,1)S(1)} fusion(bf16[2048,1024]{1,0:T(8,128)(2,1)} %all-gather.10.cloned.1.call-done, bf16[2,1024,768]{2,1,0:T(8,128)(2,1)} %param.14), kind=kOutput, calls=%fused_computation.51 | convolution fusion | flops 3222798336 | bytes 8912896 | tf_op jit(solution)/shard_map/dot_general | solution.py:75
  179.7 1.5 collective-permute-start
  181.3 3.3 %collective-permute-start.1 = (bf16[512,512]{0,1:T(8,128)(2,1)S(1)}, bf16[512,512]{0,1:T(8,128)(2,1)S(1)}, u32[]{:S(2)}, u32[]{:S(2)}) collective-permute-start(bf16[512,512]{0,1:T(8,128)(2,1)S(1)} %bitcast.97), channel_id=1, source_target_pairs={{4,0},{8,4},{12,8},{16,12},{20,16},{24,20},{28,24},{0,28},{5,1},{9... | collective-permute-start | bytes 1572872 | tf_op jit(solution)/shard_map/ppermute | solution.py:19
  184.8 1.1 slice_bitcast_fusion.2
  185.9 18.2 %collective-permute-done = bf16[512,512]{0,1:T(8,128)(2,1)S(1)} collective-permute-done((bf16[512,512]{0,1:T(8,128)(2,1)S(1)}, bf16[512,512]{0,1:T(8,128)(2,1)S(1)}, u32[]{:S(2)}, u32[]{:S(2)}) %collective-permute-start) | collective-permute-done | bytes 524320 | tf_op jit(solution)/shard_map/ppermute | solution.py:18
  204.1 2.2 collective-permute-done.1
  206.6 1.4 slice_bitcast_fusion
  208.1 1.1 broadcast.125
  209.1 58.0 %while.25 = (s32[]{:T(128)}, bf16[4,512,4,64]{1,3,2,0:T(8,128)(2,1)}, s32[4]{0:T(128)S(1)}, bf16[3072,4,64]{0,2,1:T(8,128)(2,1)}, s32[2048]{0:T(1024)S(1)}, /*in...) while((s32[]{:T(128)}, ...), condition=%wide.region_11.12_spmd, body=%wide.region_8.11_spmd.sunk | while | flops 550110208 | bytes 19434436 | solution.py:62
  209.1 0.6 dynamic_slice.142
  210.5 0.4 broadcast_compare_fusion.5
  210.9 7.0 %fusion.128 = (f32[4,512]{1,0:T(4,128)S(1)}, f32[4,512,1024]{2,1,0:T(8,128)}) fusion(pred[512,1024]{1,0:T(8,128)(4,1)S(1)} %broadcast_compare_fusion.5, bf16[3072,4,64]{0,2,1:T(8,128)(2,1)S(1)} %get-tuple-element.436, s32[]{:T(128)S(6)} %select_n.103, bf16[2048,4,64]{0,2,1:T(8,128)(2,1)} %get-tuple-element.435, s32[]{:T(128)S(6)} %select_n.104), kind=kOutput, calls=%fused_computation.94.clone.1 | convolution fusion | flops 276825088 | bytes 9707528 | tf_op jit(solution)/shard_map/while/body/eval_jaxpr/sub | solution.py:57
  217.9 5.7 %fusion.129 = bf16[4,512,4,64]{1,3,2,0:T(8,128)(2,1)} fusion(bf16[4,512,4,64]{1,3,2,0:T(8,128)(2,1)} %get-tuple-element.412, s32[]{:T(128)} %get-tuple-element.411, f32[4,512,1024]{2,1,0:T(8,128)} %get-tuple-element.346, f32[4,512]{1,0:T(4,128)S(1)} %get-tuple-element.347, bf16[3072,4,64]{0,2,1:T(8,128)(2,1)} %get-tuple-element.432, s32[]{:T(128)S(6)} %select_n.103), kind=kOutput, calls=%fused_computation.37.clone.1 | convolution fusion | flops 272760832 | bytes 9183748 | tf_op jit(solution)/shard_map/while/body/eval_jaxpr/hqk,khd->qhd/dot_general | solution.py:59
  223.6 0.6 dynamic_slice.142
  225.0 0.4 broadcast_compare_fusion.5
  225.4 7.0 %fusion.128 = (f32[4,512]{1,0:T(4,128)S(1)}, f32[4,512,1024]{2,1,0:T(8,128)}) fusion(pred[512,1024]{1,0:T(8,128)(4,1)S(1)} %broadcast_compare_fusion.5, bf16[3072,4,64]{0,2,1:T(8,128)(2,1)S(1)} %get-tuple-element.436, s32[]{:T(128)S(6)} %select_n.103, bf16[2048,4,64]{0,2,1:T(8,128)(2,1)} %get-tuple-element.435, s32[]{:T(128)S(6)} %select_n.104), kind=kOutput, calls=%fused_computation.94.clone.1 | convolution fusion | flops 276825088 | bytes 9707528 | tf_op jit(solution)/shard_map/while/body/eval_jaxpr/sub | solution.py:57
  232.4 5.7 %fusion.129 = bf16[4,512,4,64]{1,3,2,0:T(8,128)(2,1)} fusion(bf16[4,512,4,64]{1,3,2,0:T(8,128)(2,1)} %get-tuple-element.412, s32[]{:T(128)} %get-tuple-element.411, f32[4,512,1024]{2,1,0:T(8,128)} %get-tuple-element.346, f32[4,512]{1,0:T(4,128)S(1)} %get-tuple-element.347, bf16[3072,4,64]{0,2,1:T(8,128)(2,1)} %get-tuple-element.432, s32[]{:T(128)S(6)} %select_n.103), kind=kOutput, calls=%fused_computation.37.clone.1 | convolution fusion | flops 272760832 | bytes 9183748 | tf_op jit(solution)/shard_map/while/body/eval_jaxpr/hqk,khd->qhd/dot_general | solution.py:59
  238.2 0.6 dynamic_slice.142
  239.5 0.4 broadcast_compare_fusion.5
  239.9 7.0 %fusion.128 = (f32[4,512]{1,0:T(4,128)S(1)}, f32[4,512,1024]{2,1,0:T(8,128)}) fusion(pred[512,1024]{1,0:T(8,128)(4,1)S(1)} %broadcast_compare_fusion.5, bf16[3072,4,64]{0,2,1:T(8,128)(2,1)S(1)} %get-tuple-element.436, s32[]{:T(128)S(6)} %select_n.103, bf16[2048,4,64]{0,2,1:T(8,128)(2,1)} %get-tuple-element.435, s32[]{:T(128)S(6)} %select_n.104), kind=kOutput, calls=%fused_computation.94.clone.1 | convolution fusion | flops 276825088 | bytes 9707528 | tf_op jit(solution)/shard_map/while/body/eval_jaxpr/sub | solution.py:57
  246.9 5.7 %fusion.129 = bf16[4,512,4,64]{1,3,2,0:T(8,128)(2,1)} fusion(bf16[4,512,4,64]{1,3,2,0:T(8,128)(2,1)} %get-tuple-element.412, s32[]{:T(128)} %get-tuple-element.411, f32[4,512,1024]{2,1,0:T(8,128)} %get-tuple-element.346, f32[4,512]{1,0:T(4,128)S(1)} %get-tuple-element.347, bf16[3072,4,64]{0,2,1:T(8,128)(2,1)} %get-tuple-element.432, s32[]{:T(128)S(6)} %select_n.103), kind=kOutput, calls=%fused_computation.37.clone.1 | convolution fusion | flops 272760832 | bytes 9183748 | tf_op jit(solution)/shard_map/while/body/eval_jaxpr/hqk,khd->qhd/dot_general | solution.py:59
  252.7 0.6 dynamic_slice.142
  254.0 0.4 broadcast_compare_fusion.5
  254.4 7.0 %fusion.128 = (f32[4,512]{1,0:T(4,128)S(1)}, f32[4,512,1024]{2,1,0:T(8,128)}) fusion(pred[512,1024]{1,0:T(8,128)(4,1)S(1)} %broadcast_compare_fusion.5, bf16[3072,4,64]{0,2,1:T(8,128)(2,1)S(1)} %get-tuple-element.436, s32[]{:T(128)S(6)} %select_n.103, bf16[2048,4,64]{0,2,1:T(8,128)(2,1)} %get-tuple-element.435, s32[]{:T(128)S(6)} %select_n.104), kind=kOutput, calls=%fused_computation.94.clone.1 | convolution fusion | flops 276825088 | bytes 9707528 | tf_op jit(solution)/shard_map/while/body/eval_jaxpr/sub | solution.py:57
  261.4 5.7 %fusion.129 = bf16[4,512,4,64]{1,3,2,0:T(8,128)(2,1)} fusion(bf16[4,512,4,64]{1,3,2,0:T(8,128)(2,1)} %get-tuple-element.412, s32[]{:T(128)} %get-tuple-element.411, f32[4,512,1024]{2,1,0:T(8,128)} %get-tuple-element.346, f32[4,512]{1,0:T(4,128)S(1)} %get-tuple-element.347, bf16[3072,4,64]{0,2,1:T(8,128)(2,1)} %get-tuple-element.432, s32[]{:T(128)S(6)} %select_n.103), kind=kOutput, calls=%fused_computation.37.clone.1 | convolution fusion | flops 272760832 | bytes 9183748 | tf_op jit(solution)/shard_map/while/body/eval_jaxpr/hqk,khd->qhd/dot_general | solution.py:59
  267.2 3.5 %all-to-all-start.1 = ((bf16[4,512,256]{1,2,0:T(8,128)(2,1)}), bf16[4,512,256]{1,2,0:T(8,128)(2,1)S(1)}, u32[]{:S(2)}, u32[]{:S(2)}) async-start(bf16[4,512,256]{1,2,0:T(8,128)(2,1)} %bitcast.30), calls=%async_computation.1 | async-start | bytes 2097152 | tf_op jit(solution)/shard_map/all_to_all | solution.py:106
  270.7 14.4 %all-to-all-done.1 = bf16[4,512,256]{1,2,0:T(8,128)(2,1)S(1)} async-done(((bf16[4,512,256]{1,2,0:T(8,128)(2,1)}), bf16[4,512,256]{1,2,0:T(8,128)(2,1)S(1)}, u32[]{:S(2)}, u32[]{:S(2)}) %all-to-all-start.1) | async-done | bytes 1048608 | tf_op jit(solution)/shard_map/all_to_all | solution.py:106
  285.1 3.9 %fusion.71 = bf16[512,1024]{1,0:T(8,128)(2,1)} fusion(bf16[512,1024]{1,0:T(8,128)(2,1)S(1)} %get-tuple-element.247, bf16[512,1024]{0,1:T(8,128)(2,1)S(1)} %bitcast.94, bf16[1,1024,1024]{2,1,0:T(8,128)(2,1)} %all-gather.14.cloned.1.call-done), kind=kOutput, calls=%fused_computation.71 | convolution fusion | flops 1075314688 | bytes 5242880 | tf_op jit(solution)/shard_map/dot_general | solution.py:107
  (52 shorter events, 2.1 us)
Async XLA Ops:
  6.5 1.2 copy-start
  6.5 42.7 %all-gather.8.cloned.1.call-start = ((), (), s32[]{:S(2)}) async-start(), calls=%async_computation.2 | async-start | bytes 5242880 | tf_op jit(solution)/shard_map/all_gather | solution.py:76
  7.8 2.7 copy-start.3
  9.8 2.1 copy-start.2
  10.5 2.6 copy-start.4
  11.9 108.1 %all-gather.12.cloned.1.call-start = ((), (), s32[]{:S(2)}) async-start(), calls=%async_computation.4 | async-start | bytes 2621440 | tf_op jit(solution)/shard_map/all_gather | solution.py:109
  116.2 17.9 %all-to-all-start = ((bf16[4,512,256]{1,2,0:T(8,128)(2,1)}), bf16[4,512,256]{1,2,0:T(8,128)(2,1)S(1)}, u32[]{:S(2)}, u32[]{:S(2)}) async-start(bf16[4,512,256]{1,2,0:T(8,128)(2,1)} %bitcast.16), calls=%async_computation | async-start | bytes 2097152 | tf_op jit(solution)/shard_map/all_to_all | solution.py:106
  119.7 53.8 %all-gather.10.cloned.1.call-start = ((), (), s32[]{:S(2)}) async-start(), calls=%async_computation.3 | async-start | bytes 5242880 | tf_op jit(solution)/shard_map/all_gather | solution.py:76
  138.9 131.8 %all-gather.14.cloned.1.call-start = ((), (), s32[]{:S(2)}) async-start(), calls=%async_computation.5 | async-start | bytes 2621440 | tf_op jit(solution)/shard_map/all_gather | solution.py:109
  139.0 45.6 %collective-permute-start.2 = (bf16[512]{0:T(512)(128)(2,1)S(1)}, bf16[512]{0:T(512)(128)(2,1)S(1)}, u32[]{:S(2)}, u32[]{:S(2)}) collective-permute-start(bf16[512]{0:T(512)(128)(2,1)S(1)} %get-tuple-element.244), channel_id=1, source_target_pairs={{0,4},{4,8},{8,12},{12,16},{16,20},{20,24},{24,28},{28,0},{1,5},{5... | collective-permute-start | bytes 3080 | tf_op jit(solution)/shard_map/ppermute | solution.py:18
  140.5 44.1 %collective-permute-start.3 = (bf16[512]{0:T(512)(128)(2,1)S(1)}, bf16[512]{0:T(512)(128)(2,1)S(1)}, u32[]{:S(2)}, u32[]{:S(2)}) collective-permute-start(bf16[512]{0:T(512)(128)(2,1)S(1)} %get-tuple-element.245), channel_id=1, source_target_pairs={{4,0},{8,4},{12,8},{16,12},{20,16},{24,20},{28,24},{0,28},{5,1},{9... | collective-permute-start | bytes 3080 | tf_op jit(solution)/shard_map/ppermute | solution.py:19
  179.7 24.3 %collective-permute-start = (bf16[512,512]{0,1:T(8,128)(2,1)S(1)}, bf16[512,512]{0,1:T(8,128)(2,1)S(1)}, u32[]{:S(2)}, u32[]{:S(2)}) collective-permute-start(bf16[512,512]{0,1:T(8,128)(2,1)S(1)} %bitcast.98), channel_id=1, source_target_pairs={{0,4},{4,8},{8,12},{12,16},{16,20},{20,24},{24,28},{28,0},{1,5},{5... | collective-permute-start | bytes 1572872 | tf_op jit(solution)/shard_map/ppermute | solution.py:18
  181.3 25.0 %collective-permute-start.1 = (bf16[512,512]{0,1:T(8,128)(2,1)S(1)}, bf16[512,512]{0,1:T(8,128)(2,1)S(1)}, u32[]{:S(2)}, u32[]{:S(2)}) collective-permute-start(bf16[512,512]{0,1:T(8,128)(2,1)S(1)} %bitcast.97), channel_id=1, source_target_pairs={{4,0},{8,4},{12,8},{16,12},{20,16},{24,20},{28,24},{0,28},{5,1},{9... | collective-permute-start | bytes 1572872 | tf_op jit(solution)/shard_map/ppermute | solution.py:19
  267.2 17.9 %all-to-all-start.1 = ((bf16[4,512,256]{1,2,0:T(8,128)(2,1)}), bf16[4,512,256]{1,2,0:T(8,128)(2,1)S(1)}, u32[]{:S(2)}, u32[]{:S(2)}) async-start(bf16[4,512,256]{1,2,0:T(8,128)(2,1)} %bitcast.30), calls=%async_computation.1 | async-start | bytes 2097152 | tf_op jit(solution)/shard_map/all_to_all | solution.py:106
  285.1 3.9 %copy-start.1 = (bf16[512,1024]{1,0:T(8,128)(2,1)S(1)}, bf16[512,1024]{1,0:T(8,128)(2,1)}, u32[]{:S(2)}) copy-start(bf16[512,1024]{1,0:T(8,128)(2,1)} %param.10) | copy-start | bytes 3145732
Sparse Core Ops, SparseCore 0:
  12.0 37.1 all-gather.7
  50.8 22.5 all-gather.11
  139.0 34.4 all-gather.9
  174.9 22.5 all-gather.13
where the time goes:
time: 296 us
  matrix products  121 us (41%)
  waiting for transfers between devices  109 us (37%)
  starting transfers between devices  16.9 us (6%)
  local copies, waits for them, and re-layouts  15.9 us (5%)
  between operations  13.3 us (4%)
  other arithmetic  7.79 us (3%)
  blocking collectives  6.2 us (2%)
  loops' own time  5.57 us (2%)
    all_gather x2, waiting for transfers between devices, on_device(): lax.all_gather(normed, 'head', axis=0, tiled=True)  59.7 us
    sub x8, matrix products, one_block(): expo = jnp.exp(scores - row_max)  56.2 us
    dot_general x8, matrix products, one_block(): jnp.einsum('hqk,khd->qhd', probs, value_block, preferred_element_type=jnp...  45.9 us
    all_to_all x2, waiting for transfers between devices, on_device(): lax.all_to_all(attended, 'head', split_axis=0, concat_axis=1, tiled=True)  28.5 us
    ppermute x2, waiting for transfers between devices, extended(): before = lax.ppermute(last, axis, up)  18.2 us
    dot_general x2, matrix products, on_device(): jnp.dot(lax.all_gather(normed, 'head', axis=0, tiled=True), weights_here,...  12.3 us
    all_to_all x2, starting transfers between devices, on_device(): lax.all_to_all(attended, 'head', split_axis=0, concat_axis=1, tiled=True)  7.03 us
    dot_general x2, matrix products, on_device(): jnp.dot(heads_rows, lax.all_gather(w_out[layer_index], 'head', axis=0, ti...  6.86 us
  transfers between devices with their start and end apart: 10, of which 6 were waited for; matrix products, arithmetic and copies ran while one was open for 44% of the time, Pallas kernels for 0%

commit v1 on v0

--- a/solution.py
+++ b/solution.py
@@ -73,7 +73,9 @@
         normed = layer_norm(stream, ln_gain[layer_index])
         weights_here = w_qkv[layer_index]
         qkv_span = jnp.dot(
-            lax.all_gather(normed, "head", axis=0, tiled=True),
+            jnp.concatenate(
+                lax.all_to_all(jnp.stack([normed] * lax.axis_size("head")), "head", 0, 0), axis=0
+            ),
             weights_here,
             preferred_element_type=jnp.float32,
         ).astype(jnp.bfloat16)

time: 296 us -> 359 us (1.21)
  blocking collectives: 6.2 us -> 59.9 us
  starting transfers between devices: 16.9 us -> 27.9 us
  waiting for transfers between devices: 109 us -> 103 us
  local copies, waits for them, and re-layouts: 15.9 us -> 20.4 us
    all_gather x2 -> x0, waiting for transfers between devices: 59.7 us -> none  [on_device(): lax.all_gather(normed, 'head', axis=0, tiled=True)]
    all_to_all x0 -> x2, waiting for transfers between devices: none -> 53.9 us  [on_device(): lax.all_to_all(jnp.stack([normed] * lax.axis_size('head')), 'head', 0, 0)]
    all_gather x1, blocking collectives: 6.2 us -> 59.9 us  [on_device(): range_ids = lax.all_gather(scan_ids, 'head', axis=0, tiled=True)]
    all_to_all x0 -> x2, starting transfers between devices: none -> 9.82 us  [on_device(): lax.all_to_all(jnp.stack([normed] * lax.axis_size('head')), 'head', 0, 0)]
    another operation x2 -> x4, local copies, waits for them, and re-layouts: 2.15 us -> 7.18 us  [the longest x2 5.04 us: on_device(): jnp.stack([normed] * lax.axis_size('head'))]
  transfers between devices with their start and end apart: 10 -> 10, of which waited for: 6 -> 5; matrix products, arithmetic and copies ran while one was open for 44% -> 37% of each run, Pallas kernels for 0% -> 0%
where the time goes in v1:
time: 359 us; the launch traced here: 358 us
  matrix products  122 us (34%)
  waiting for transfers between devices  103 us (29%)
  blocking collectives  59.9 us (17%)
  starting transfers between devices  27.9 us (8%)
  local copies, waits for them, and re-layouts  20.4 us (6%)
  between operations  13.6 us (4%)
  other arithmetic  5.85 us (2%)
  loops' own time  5.56 us (2%)
    all_gather x1, blocking collectives, on_device(): range_ids = lax.all_gather(scan_ids, 'head', axis=0, tiled=True)  59.9 us
    sub x8, matrix products, one_block(): expo = jnp.exp(scores - row_max)  56.7 us
    all_to_all x2, waiting for transfers between devices, on_device(): lax.all_to_all(jnp.stack([normed] * lax.axis_size('head')), 'head', 0, 0)  53.9 us
    dot_general x8, matrix products, one_block(): jnp.einsum('hqk,khd->qhd', probs, value_block, preferred_element_type=jnp...  45.9 us
    all_to_all x2, waiting for transfers between devices, on_device(): lax.all_to_all(attended, 'head', split_axis=0, concat_axis=1, tiled=True)  28.6 us
    ppermute x2, waiting for transfers between devices, extended(): before = lax.ppermute(last, axis, up)  18.7 us
    dot_general x2, matrix products, on_device(): jnp.dot(jnp.concatenate(lax.all_to_all(jnp.stack([normed] * lax.axis_size...  12.3 us
    all_to_all x2, starting transfers between devices, on_device(): lax.all_to_all(jnp.stack([normed] * lax.axis_size('head')), 'head', 0, 0)  9.82 us
  transfers between devices with their start and end apart: 10, of which 5 were waited for; matrix products, arithmetic and copies ran while one was open for 37% of the time, Pallas kernels for 0%

profile of v1, /device:TPU:0, one launch (start us, length us, event | category | flops | bytes accessed | tf_op | source)
XLA Modules:
  0.0 358.3 jit_solution(17093716993064580837)
XLA Ops:
  6.5 0.8 compare_select_fusion
  7.3 0.5 copy-done
  7.8 2.0 gather_fusion
  10.1 0.4 fusion.67
  10.5 0.4 fusion.69
  10.9 2.5 stack.4
  13.4 5.0 %all-to-all-start = ((bf16[4,512,1024]{2,1,0:T(8,128)(2,1)}), bf16[4,512,1024]{2,1,0:T(8,128)(2,1)}, u32[]{:S(2)}, u32[]{:S(2)}) async-start(bf16[4,512,1024]{2,1,0:T(8,128)(2,1)} %stack.4), calls=%async_computation | async-start | bytes 8388608 | tf_op jit(solution)/shard_map/all_to_all | solution.py:77
  18.5 1.1 fusion.103
  19.6 59.9 %all-gather.2 = s32[4,1,512]{2,1,0:T(1,128)S(1)} all-gather(s32[1,1,512]{2,1,0:T(1,128)S(1)} %bitcast.105), channel_id=1, replica_groups=mesh['curve'=8,'head'=4] {'head'}, dimensions={0}, use_global_device_ids=true | all-gather | bytes 10240 | tf_op jit(solution)/shard_map/all_gather | solution.py:68
  79.4 6.1 %convolution_convert_fusion.1 = bf16[2048,768]{0,1:T(8,128)(2,1)S(1)} fusion(bf16[2048,1024]{1,0:T(8,128)(2,1)} %bitcast.9, bf16[2,1024,768]{2,1,0:T(8,128)(2,1)} %param.14), kind=kOutput, calls=%fused_computation.52 | convolution fusion | flops 3222798336 | bytes 8912896 | tf_op jit(solution)/shard_map/dot_general | solution.py:75
  85.6 1.7 slice_bitcast_fusion.3
  87.2 1.1 broadcast.139.clone
  88.3 58.1 %while.24 = (s32[]{:T(128)}, bf16[4,512,4,64]{1,3,2,0:T(8,128)(2,1)}, s32[4]{0:T(128)S(1)}, bf16[2048,4,64]{0,2,1:T(8,128)(2,1)}, s32[2048]{0:T(1024)S(1)}, /*in...) while((s32[]{:T(128)}, ...), condition=%wide.region_5.6_spmd, body=%wide.region_2.5_spmd.sunk | while | flops 550110208 | bytes 19434388 | solution.py:62
  88.3 0.6 dynamic_slice.136
  89.7 0.4 broadcast_compare_fusion.4
  90.0 7.0 %fusion.123 = (f32[4,512]{1,0:T(4,128)S(1)}, f32[4,512,1024]{2,1,0:T(8,128)}) fusion(pred[512,1024]{1,0:T(8,128)(4,1)S(1)} %broadcast_compare_fusion.4, bf16[2048,4,64]{0,2,1:T(8,128)(2,1)S(1)} %get-tuple-element.384, s32[]{:T(128)S(6)} %select_n.99, bf16[2048,4,64]{0,2,1:T(8,128)(2,1)} %get-tuple-element.383, s32[]{:T(128)S(6)} %select_n.100), kind=kOutput, calls=%fused_computation.93.clone.1 | convolution fusion | flops 276825088 | bytes 9707528 | tf_op jit(solution)/shard_map/while/body/eval_jaxpr/sub | solution.py:57
  97.1 5.7 %fusion.124 = bf16[4,512,4,64]{1,3,2,0:T(8,128)(2,1)} fusion(bf16[4,512,4,64]{1,3,2,0:T(8,128)(2,1)} %get-tuple-element.364, s32[]{:T(128)} %get-tuple-element.363, f32[4,512,1024]{2,1,0:T(8,128)} %get-tuple-element.336, f32[4,512]{1,0:T(4,128)S(1)} %get-tuple-element.337, bf16[2048,4,64]{0,2,1:T(8,128)(2,1)} %get-tuple-element.381, s32[]{:T(128)S(6)} %select_n.99), kind=kOutput, calls=%fused_computation.12.clone.1 | convolution fusion | flops 272760832 | bytes 9183748 | tf_op jit(solution)/shard_map/while/body/eval_jaxpr/hqk,khd->qhd/dot_general | solution.py:59
  102.8 0.6 dynamic_slice.136
  104.2 0.4 broadcast_compare_fusion.4
  104.6 7.0 %fusion.123 = (f32[4,512]{1,0:T(4,128)S(1)}, f32[4,512,1024]{2,1,0:T(8,128)}) fusion(pred[512,1024]{1,0:T(8,128)(4,1)S(1)} %broadcast_compare_fusion.4, bf16[2048,4,64]{0,2,1:T(8,128)(2,1)S(1)} %get-tuple-element.384, s32[]{:T(128)S(6)} %select_n.99, bf16[2048,4,64]{0,2,1:T(8,128)(2,1)} %get-tuple-element.383, s32[]{:T(128)S(6)} %select_n.100), kind=kOutput, calls=%fused_computation.93.clone.1 | convolution fusion | flops 276825088 | bytes 9707528 | tf_op jit(solution)/shard_map/while/body/eval_jaxpr/sub | solution.py:57
  111.6 5.7 %fusion.124 = bf16[4,512,4,64]{1,3,2,0:T(8,128)(2,1)} fusion(bf16[4,512,4,64]{1,3,2,0:T(8,128)(2,1)} %get-tuple-element.364, s32[]{:T(128)} %get-tuple-element.363, f32[4,512,1024]{2,1,0:T(8,128)} %get-tuple-element.336, f32[4,512]{1,0:T(4,128)S(1)} %get-tuple-element.337, bf16[2048,4,64]{0,2,1:T(8,128)(2,1)} %get-tuple-element.381, s32[]{:T(128)S(6)} %select_n.99), kind=kOutput, calls=%fused_computation.12.clone.1 | convolution fusion | flops 272760832 | bytes 9183748 | tf_op jit(solution)/shard_map/while/body/eval_jaxpr/hqk,khd->qhd/dot_general | solution.py:59
  117.3 0.6 dynamic_slice.136
  118.7 0.4 broadcast_compare_fusion.4
  119.1 7.0 %fusion.123 = (f32[4,512]{1,0:T(4,128)S(1)}, f32[4,512,1024]{2,1,0:T(8,128)}) fusion(pred[512,1024]{1,0:T(8,128)(4,1)S(1)} %broadcast_compare_fusion.4, bf16[2048,4,64]{0,2,1:T(8,128)(2,1)S(1)} %get-tuple-element.384, s32[]{:T(128)S(6)} %select_n.99, bf16[2048,4,64]{0,2,1:T(8,128)(2,1)} %get-tuple-element.383, s32[]{:T(128)S(6)} %select_n.100), kind=kOutput, calls=%fused_computation.93.clone.1 | convolution fusion | flops 276825088 | bytes 9707528 | tf_op jit(solution)/shard_map/while/body/eval_jaxpr/sub | solution.py:57
  126.1 5.7 %fusion.124 = bf16[4,512,4,64]{1,3,2,0:T(8,128)(2,1)} fusion(bf16[4,512,4,64]{1,3,2,0:T(8,128)(2,1)} %get-tuple-element.364, s32[]{:T(128)} %get-tuple-element.363, f32[4,512,1024]{2,1,0:T(8,128)} %get-tuple-element.336, f32[4,512]{1,0:T(4,128)S(1)} %get-tuple-element.337, bf16[2048,4,64]{0,2,1:T(8,128)(2,1)} %get-tuple-element.381, s32[]{:T(128)S(6)} %select_n.99), kind=kOutput, calls=%fused_computation.12.clone.1 | convolution fusion | flops 272760832 | bytes 9183748 | tf_op jit(solution)/shard_map/while/body/eval_jaxpr/hqk,khd->qhd/dot_general | solution.py:59
  131.8 0.6 dynamic_slice.136
  133.2 0.4 broadcast_compare_fusion.4
  133.6 7.0 %fusion.123 = (f32[4,512]{1,0:T(4,128)S(1)}, f32[4,512,1024]{2,1,0:T(8,128)}) fusion(pred[512,1024]{1,0:T(8,128)(4,1)S(1)} %broadcast_compare_fusion.4, bf16[2048,4,64]{0,2,1:T(8,128)(2,1)S(1)} %get-tuple-element.384, s32[]{:T(128)S(6)} %select_n.99, bf16[2048,4,64]{0,2,1:T(8,128)(2,1)} %get-tuple-element.383, s32[]{:T(128)S(6)} %select_n.100), kind=kOutput, calls=%fused_computation.93.clone.1 | convolution fusion | flops 276825088 | bytes 9707528 | tf_op jit(solution)/shard_map/while/body/eval_jaxpr/sub | solution.py:57
  140.6 5.7 %fusion.124 = bf16[4,512,4,64]{1,3,2,0:T(8,128)(2,1)} fusion(bf16[4,512,4,64]{1,3,2,0:T(8,128)(2,1)} %get-tuple-element.364, s32[]{:T(128)} %get-tuple-element.363, f32[4,512,1024]{2,1,0:T(8,128)} %get-tuple-element.336, f32[4,512]{1,0:T(4,128)S(1)} %get-tuple-element.337, bf16[2048,4,64]{0,2,1:T(8,128)(2,1)} %get-tuple-element.381, s32[]{:T(128)S(6)} %select_n.99), kind=kOutput, calls=%fused_computation.12.clone.1 | convolution fusion | flops 272760832 | bytes 9183748 | tf_op jit(solution)/shard_map/while/body/eval_jaxpr/hqk,khd->qhd/dot_general | solution.py:59
  146.4 3.7 %all-to-all-start.1 = ((bf16[4,512,256]{1,2,0:T(8,128)(2,1)}), bf16[4,512,256]{1,2,0:T(8,128)(2,1)S(1)}, u32[]{:S(2)}, u32[]{:S(2)}) async-start(bf16[4,512,256]{1,2,0:T(8,128)(2,1)} %bitcast.17), calls=%async_computation.1 | async-start | bytes 2097152 | tf_op jit(solution)/shard_map/all_to_all | solution.py:108
  150.1 14.2 %all-to-all-done.1 = bf16[4,512,256]{1,2,0:T(8,128)(2,1)S(1)} async-done(((bf16[4,512,256]{1,2,0:T(8,128)(2,1)}), bf16[4,512,256]{1,2,0:T(8,128)(2,1)S(1)}, u32[]{:S(2)}, u32[]{:S(2)}) %all-to-all-start.1) | async-done | bytes 1048608 | tf_op jit(solution)/shard_map/all_to_all | solution.py:108
  164.3 2.9 convert_reduce_fusion
  167.2 0.4 fusion.64
  167.7 0.4 fusion.66
  168.1 2.5 stack.5
  170.6 4.8 %all-to-all-start.2 = ((bf16[4,512,1024]{2,1,0:T(8,128)(2,1)}), bf16[4,512,1024]{2,1,0:T(8,128)(2,1)}, u32[]{:S(2)}, u32[]{:S(2)}) async-start(bf16[4,512,1024]{2,1,0:T(8,128)(2,1)} %stack.5), calls=%async_computation.2 | async-start | bytes 8388608 | tf_op jit(solution)/shard_map/all_to_all | solution.py:77
  175.5 2.3 collective-permute-start.2
  177.8 3.1 collective-permute-start.3
  180.9 53.9 %all-to-all-done.2 = bf16[4,512,1024]{2,1,0:T(8,128)(2,1)} async-done(((bf16[4,512,1024]{2,1,0:T(8,128)(2,1)}), bf16[4,512,1024]{2,1,0:T(8,128)(2,1)}, u32[]{:S(2)}, u32[]{:S(2)}) %all-to-all-start.2) | async-done | bytes 4194336 | tf_op jit(solution)/shard_map/all_to_all | solution.py:77
  234.9 6.1 %convolution_convert_fusion = bf16[2048,768]{0,1:T(8,128)(2,1)S(1)} fusion(bf16[2048,1024]{1,0:T(8,128)(2,1)} %bitcast.22, bf16[2,1024,768]{2,1,0:T(8,128)(2,1)} %param.14), kind=kOutput, calls=%fused_computation.51 | convolution fusion | flops 3222798336 | bytes 8912896 | tf_op jit(solution)/shard_map/dot_general | solution.py:75
  241.1 2.3 collective-permute-start
  243.4 3.1 collective-permute-start.1
  246.9 18.7 %collective-permute-done = bf16[512,512]{0,1:T(8,128)(2,1)S(1)} collective-permute-done((bf16[512,512]{0,1:T(8,128)(2,1)S(1)}, bf16[512,512]{0,1:T(8,128)(2,1)S(1)}, u32[]{:S(2)}, u32[]{:S(2)}) %collective-permute-start) | collective-permute-done | bytes 524320 | tf_op jit(solution)/shard_map/ppermute | solution.py:18
  265.5 2.2 collective-permute-done.1
  268.1 2.0 slice_bitcast_fusion
  270.1 1.1 broadcast.139
  271.2 58.5 %while.25 = (s32[]{:T(128)}, bf16[4,512,4,64]{1,3,2,0:T(8,128)(2,1)}, s32[4]{0:T(128)S(1)}, bf16[3072,4,64]{0,2,1:T(8,128)(2,1)}, s32[2048]{0:T(1024)S(1)}, /*in...) while((s32[]{:T(128)}, ...), condition=%wide.region_11.12_spmd, body=%wide.region_8.11_spmd.sunk | while | flops 550110208 | bytes 19434436 | solution.py:62
  271.2 0.6 dynamic_slice.142
  272.6 0.4 broadcast_compare_fusion.5
  272.9 7.1 %fusion.128 = (f32[4,512]{1,0:T(4,128)S(1)}, f32[4,512,1024]{2,1,0:T(8,128)}) fusion(pred[512,1024]{1,0:T(8,128)(4,1)S(1)} %broadcast_compare_fusion.5, bf16[3072,4,64]{0,2,1:T(8,128)(2,1)} %get-tuple-element.436, s32[]{:T(128)S(6)} %select_n.103, bf16[2048,4,64]{0,2,1:T(8,128)(2,1)S(1)} %get-tuple-element.435, s32[]{:T(128)S(6)} %select_n.104), kind=kOutput, calls=%fused_computation.94.clone.1 | convolution fusion | flops 276825088 | bytes 9707528 | tf_op jit(solution)/shard_map/while/body/eval_jaxpr/sub | solution.py:57
  280.1 5.7 %fusion.129 = bf16[4,512,4,64]{1,3,2,0:T(8,128)(2,1)} fusion(bf16[4,512,4,64]{1,3,2,0:T(8,128)(2,1)} %get-tuple-element.412, s32[]{:T(128)} %get-tuple-element.411, f32[4,512,1024]{2,1,0:T(8,128)} %get-tuple-element.346, f32[4,512]{1,0:T(4,128)S(1)} %get-tuple-element.347, bf16[3072,4,64]{0,2,1:T(8,128)(2,1)} %get-tuple-element.432, s32[]{:T(128)S(6)} %select_n.103), kind=kOutput, calls=%fused_computation.37.clone.1 | convolution fusion | flops 272760832 | bytes 9183748 | tf_op jit(solution)/shard_map/while/body/eval_jaxpr/hqk,khd->qhd/dot_general | solution.py:59
  285.8 0.6 dynamic_slice.142
  287.2 0.4 broadcast_compare_fusion.5
  287.5 7.1 %fusion.128 = (f32[4,512]{1,0:T(4,128)S(1)}, f32[4,512,1024]{2,1,0:T(8,128)}) fusion(pred[512,1024]{1,0:T(8,128)(4,1)S(1)} %broadcast_compare_fusion.5, bf16[3072,4,64]{0,2,1:T(8,128)(2,1)} %get-tuple-element.436, s32[]{:T(128)S(6)} %select_n.103, bf16[2048,4,64]{0,2,1:T(8,128)(2,1)S(1)} %get-tuple-element.435, s32[]{:T(128)S(6)} %select_n.104), kind=kOutput, calls=%fused_computation.94.clone.1 | convolution fusion | flops 276825088 | bytes 9707528 | tf_op jit(solution)/shard_map/while/body/eval_jaxpr/sub | solution.py:57
  294.7 5.7 %fusion.129 = bf16[4,512,4,64]{1,3,2,0:T(8,128)(2,1)} fusion(bf16[4,512,4,64]{1,3,2,0:T(8,128)(2,1)} %get-tuple-element.412, s32[]{:T(128)} %get-tuple-element.411, f32[4,512,1024]{2,1,0:T(8,128)} %get-tuple-element.346, f32[4,512]{1,0:T(4,128)S(1)} %get-tuple-element.347, bf16[3072,4,64]{0,2,1:T(8,128)(2,1)} %get-tuple-element.432, s32[]{:T(128)S(6)} %select_n.103), kind=kOutput, calls=%fused_computation.37.clone.1 | convolution fusion | flops 272760832 | bytes 9183748 | tf_op jit(solution)/shard_map/while/body/eval_jaxpr/hqk,khd->qhd/dot_general | solution.py:59
  300.4 0.6 dynamic_slice.142
  302.2 7.1 %fusion.128 = (f32[4,512]{1,0:T(4,128)S(1)}, f32[4,512,1024]{2,1,0:T(8,128)}) fusion(pred[512,1024]{1,0:T(8,128)(4,1)S(1)} %broadcast_compare_fusion.5, bf16[3072,4,64]{0,2,1:T(8,128)(2,1)} %get-tuple-element.436, s32[]{:T(128)S(6)} %select_n.103, bf16[2048,4,64]{0,2,1:T(8,128)(2,1)S(1)} %get-tuple-element.435, s32[]{:T(128)S(6)} %select_n.104), kind=kOutput, calls=%fused_computation.94.clone.1 | convolution fusion | flops 276825088 | bytes 9707528 | tf_op jit(solution)/shard_map/while/body/eval_jaxpr/sub | solution.py:57
  309.3 5.7 %fusion.129 = bf16[4,512,4,64]{1,3,2,0:T(8,128)(2,1)} fusion(bf16[4,512,4,64]{1,3,2,0:T(8,128)(2,1)} %get-tuple-element.412, s32[]{:T(128)} %get-tuple-element.411, f32[4,512,1024]{2,1,0:T(8,128)} %get-tuple-element.346, f32[4,512]{1,0:T(4,128)S(1)} %get-tuple-element.347, bf16[3072,4,64]{0,2,1:T(8,128)(2,1)} %get-tuple-element.432, s32[]{:T(128)S(6)} %select_n.103), kind=kOutput, calls=%fused_computation.37.clone.1 | convolution fusion | flops 272760832 | bytes 9183748 | tf_op jit(solution)/shard_map/while/body/eval_jaxpr/hqk,khd->qhd/dot_general | solution.py:59
  315.0 0.6 dynamic_slice.142
  316.8 7.1 %fusion.128 = (f32[4,512]{1,0:T(4,128)S(1)}, f32[4,512,1024]{2,1,0:T(8,128)}) fusion(pred[512,1024]{1,0:T(8,128)(4,1)S(1)} %broadcast_compare_fusion.5, bf16[3072,4,64]{0,2,1:T(8,128)(2,1)} %get-tuple-element.436, s32[]{:T(128)S(6)} %select_n.103, bf16[2048,4,64]{0,2,1:T(8,128)(2,1)S(1)} %get-tuple-element.435, s32[]{:T(128)S(6)} %select_n.104), kind=kOutput, calls=%fused_computation.94.clone.1 | convolution fusion | flops 276825088 | bytes 9707528 | tf_op jit(solution)/shard_map/while/body/eval_jaxpr/sub | solution.py:57
  323.9 5.7 %fusion.129 = bf16[4,512,4,64]{1,3,2,0:T(8,128)(2,1)} fusion(bf16[4,512,4,64]{1,3,2,0:T(8,128)(2,1)} %get-tuple-element.412, s32[]{:T(128)} %get-tuple-element.411, f32[4,512,1024]{2,1,0:T(8,128)} %get-tuple-element.346, f32[4,512]{1,0:T(4,128)S(1)} %get-tuple-element.347, bf16[3072,4,64]{0,2,1:T(8,128)(2,1)} %get-tuple-element.432, s32[]{:T(128)S(6)} %select_n.103), kind=kOutput, calls=%fused_computation.37.clone.1 | convolution fusion | flops 272760832 | bytes 9183748 | tf_op jit(solution)/shard_map/while/body/eval_jaxpr/hqk,khd->qhd/dot_general | solution.py:59
  329.6 3.5 all-to-all-start.3
  333.2 14.4 %all-to-all-done.3 = bf16[4,512,256]{1,2,0:T(8,128)(2,1)S(1)} async-done(((bf16[4,512,256]{1,2,0:T(8,128)(2,1)}), bf16[4,512,256]{1,2,0:T(8,128)(2,1)S(1)}, u32[]{:S(2)}, u32[]{:S(2)}) %all-to-all-start.3) | async-done | bytes 1048608 | tf_op jit(solution)/shard_map/all_to_all | solution.py:108
  347.6 3.9 %fusion.71 = bf16[512,1024]{1,0:T(8,128)(2,1)} fusion(bf16[512,1024]{1,0:T(8,128)(2,1)S(1)} %get-tuple-element.247, bf16[512,1024]{0,1:T(8,128)(2,1)S(1)} %bitcast.96, bf16[1,1024,1024]{2,1,0:T(8,128)(2,1)} %all-gather.8.cloned.1.call-done), kind=kOutput, calls=%fused_computation.71 | convolution fusion | flops 1075314688 | bytes 5242880 | tf_op jit(solution)/shard_map/dot_general | solution.py:109
  (52 shorter events, 2.6 us)
Async XLA Ops:
  6.5 1.2 copy-start
  7.8 2.7 copy-start.3
  13.4 5.0 %copy-start.2 = (bf16[2,256,1024]{2,1,0:T(8,128)(2,1)S(1)}, bf16[2,256,1024]{2,1,0:T(8,128)(2,1)}, u32[]{:S(2)}) copy-start(bf16[2,256,1024]{2,1,0:T(8,128)(2,1)} %param.15) | copy-start | bytes 3145732
  13.4 6.1 %copy-start.4 = (s32[512]{0:T(512)S(1)}, s32[512]{0:T(512)}, u32[]{:S(2)}) copy-start(s32[512]{0:T(512)} %param.12) | copy-start | bytes 6148
  13.4 66.0 %all-to-all-start = ((bf16[4,512,1024]{2,1,0:T(8,128)(2,1)}), bf16[4,512,1024]{2,1,0:T(8,128)(2,1)}, u32[]{:S(2)}, u32[]{:S(2)}) async-start(bf16[4,512,1024]{2,1,0:T(8,128)(2,1)} %stack.4), calls=%async_computation | async-start | bytes 8388608 | tf_op jit(solution)/shard_map/all_to_all | solution.py:77
  18.4 131.7 %all-gather.6.cloned.1.call-start = ((), (), s32[]{:S(2)}) async-start(), calls=%async_computation.4 | async-start | bytes 2621440 | tf_op jit(solution)/shard_map/all_gather | solution.py:111
  146.4 17.9 %all-to-all-start.1 = ((bf16[4,512,256]{1,2,0:T(8,128)(2,1)}), bf16[4,512,256]{1,2,0:T(8,128)(2,1)S(1)}, u32[]{:S(2)}, u32[]{:S(2)}) async-start(bf16[4,512,256]{1,2,0:T(8,128)(2,1)} %bitcast.17), calls=%async_computation.1 | async-start | bytes 2097152 | tf_op jit(solution)/shard_map/all_to_all | solution.py:108
  170.6 64.3 %all-to-all-start.2 = ((bf16[4,512,1024]{2,1,0:T(8,128)(2,1)}), bf16[4,512,1024]{2,1,0:T(8,128)(2,1)}, u32[]{:S(2)}, u32[]{:S(2)}) async-start(bf16[4,512,1024]{2,1,0:T(8,128)(2,1)} %stack.5), calls=%async_computation.2 | async-start | bytes 8388608 | tf_op jit(solution)/shard_map/all_to_all | solution.py:77
  175.4 157.8 %all-gather.8.cloned.1.call-start = ((), (), s32[]{:S(2)}) async-start(), calls=%async_computation.5 | async-start | bytes 2621440 | tf_op jit(solution)/shard_map/all_gather | solution.py:111
  175.5 71.0 %collective-permute-start.2 = (bf16[512]{0:T(512)(128)(2,1)S(1)}, bf16[512]{0:T(512)(128)(2,1)S(1)}, u32[]{:S(2)}, u32[]{:S(2)}) collective-permute-start(bf16[512]{0:T(512)(128)(2,1)S(1)} %get-tuple-element.244), channel_id=1, source_target_pairs={{0,4},{4,8},{8,12},{12,16},{16,20},{20,24},{24,28},{28,0},{1,5},{5... | collective-permute-start | bytes 3080 | tf_op jit(solution)/shard_map/ppermute | solution.py:18
  177.8 68.7 %collective-permute-start.3 = (bf16[512]{0:T(512)(128)(2,1)S(1)}, bf16[512]{0:T(512)(128)(2,1)S(1)}, u32[]{:S(2)}, u32[]{:S(2)}) collective-permute-start(bf16[512]{0:T(512)(128)(2,1)S(1)} %get-tuple-element.245), channel_id=1, source_target_pairs={{4,0},{8,4},{12,8},{16,12},{20,16},{24,20},{28,24},{0,28},{5,1},{9... | collective-permute-start | bytes 3080 | tf_op jit(solution)/shard_map/ppermute | solution.py:19
  241.1 24.4 %collective-permute-start = (bf16[512,512]{0,1:T(8,128)(2,1)S(1)}, bf16[512,512]{0,1:T(8,128)(2,1)S(1)}, u32[]{:S(2)}, u32[]{:S(2)}) collective-permute-start(bf16[512,512]{0,1:T(8,128)(2,1)S(1)} %bitcast.100), channel_id=1, source_target_pairs={{0,4},{4,8},{8,12},{12,16},{16,20},{20,24},{24,28},{28,0},{1,5},{5... | collective-permute-start | bytes 1572872 | tf_op jit(solution)/shard_map/ppermute | solution.py:18
  243.4 24.3 %collective-permute-start.1 = (bf16[512,512]{0,1:T(8,128)(2,1)S(1)}, bf16[512,512]{0,1:T(8,128)(2,1)S(1)}, u32[]{:S(2)}, u32[]{:S(2)}) collective-permute-start(bf16[512,512]{0,1:T(8,128)(2,1)S(1)} %bitcast.99), channel_id=1, source_target_pairs={{4,0},{8,4},{12,8},{16,12},{20,16},{24,20},{28,24},{0,28},{5,1},{9... | collective-permute-start | bytes 1572872 | tf_op jit(solution)/shard_map/ppermute | solution.py:19
  329.6 17.9 %all-to-all-start.3 = ((bf16[4,512,256]{1,2,0:T(8,128)(2,1)}), bf16[4,512,256]{1,2,0:T(8,128)(2,1)S(1)}, u32[]{:S(2)}, u32[]{:S(2)}) async-start(bf16[4,512,256]{1,2,0:T(8,128)(2,1)} %bitcast.32), calls=%async_computation.3 | async-start | bytes 2097152 | tf_op jit(solution)/shard_map/all_to_all | solution.py:108
  347.6 3.9 %copy-start.1 = (bf16[512,1024]{1,0:T(8,128)(2,1)S(1)}, bf16[512,1024]{1,0:T(8,128)(2,1)}, u32[]{:S(2)}) copy-start(bf16[512,1024]{1,0:T(8,128)(2,1)} %param.10) | copy-start | bytes 3145732
Sparse Core Ops, SparseCore 0:
  20.8 37.0 all-gather.5
  181.1 33.0 all-gather.7
